TPU v7x, 32 devices: a whole 2x2x4 slice. The times are simulated.
32 devices in a mesh: groups: 2 (over y), ga: 16 (over z, x, core).
Axes of the slice: x: 2, y: 2, z: 4, core: 2. Of those that a mesh axis runs over, the one named last changes fastest.
Arguments:
- occupied: float32 [2, 1024, 12288], P(None, None, 'ga'), may hold values from -0.0546875 to 0.0546875
- residual: float32 [4, 2, 128, 12288], P('groups', None, None, 'ga'), parts along dimension 0, may hold values from -6 to 6
- old_direction: float32 [4, 2, 128, 12288], P('groups', None, None, 'ga'), parts along dimension 0, may hold values from -6 to 6
- kin_ratio: float32 [12288], P('ga'), may hold values from 0.06 to 5, as said below
- old_dot: float32 [4, 128], P('groups'), parts along dimension 0, may hold values from 6144 to 24576
Outputs:
- direction: float32 [4, 2, 128, 12288], P('groups', None, None, 'ga'), parts along dimension 0
- dot_new: float32 [4, 128], P('groups'), parts along dimension 0
There are 2 independent parts, one for each index of `groups`. A program takes and returns all parts, laid end to end along the dimension named above; an argument that names none is the same for every part. Nothing has to cross between parts.
Inputs may be any that keep to these rules, and one draw needn't show every extreme that they name: `kin_ratio`: positive; grows with the plane-wave index on average and varies from one plane wave to the next.
All inputs are finite; a program needn't handle non-finite values.
Results may differ from a plain program's by a relative error of at most 0.000056.
Values sent between devices are 32-bit elements; how exact they have to be, the bound alone decides.
No kernel may reach another device: no remote copies, remote signals or barrier semaphores. Data moves between devices by JAX's collectives and lax.ppermute only.
A program may use at most 64 MiB of HBM per device.

v0:
```python
import jax
import jax.numpy as jnp
from jax import lax
from jax.sharding import PartitionSpec as P

highest = lax.Precision.HIGHEST


def teter_factor(ratio):
    numerator = 27.0 + 18.0 * ratio + 12.0 * ratio**2 + 8.0 * ratio**3
    return numerator / (numerator + 16.0 * ratio**4)


def margins(occupied, vectors):
    products = jnp.einsum("hng,pcbg->phcnb", occupied, vectors, precision=highest)
    real_part = products[:, 0, 0] + products[:, 1, 1]
    imag_part = products[:, 0, 1] - products[:, 1, 0]
    return jnp.stack([real_part, imag_part], axis=1)


def correction(summed, occ_rows):
    real_part = summed[:, 0]
    imag_part = summed[:, 1]
    coefficient = jnp.stack(
        [jnp.stack([real_part, -imag_part], axis=1), jnp.stack([imag_part, real_part], axis=1)],
        axis=1,
    )
    return jnp.einsum("pchnb,hng->pcbg", coefficient, occ_rows, precision=highest)


def on_device(occupied, residual, old_direction, kin_ratio, old_dot):
    factor = teter_factor(kin_ratio)
    first = margins(occupied, residual)
    first_total = lax.psum(first, "ga")
    gradient = residual - correction(first_total, occupied)
    precond = factor * gradient
    local_dot = jnp.sum(factor * (gradient[:, 0] ** 2 + gradient[:, 1] ** 2), axis=-1)
    second = margins(occupied, precond)
    second_total, dot_new = lax.psum((second, local_dot), "ga")
    projected = precond - correction(second_total, occupied)
    direction = projected + (dot_new / old_dot)[:, None, :, None] * old_direction
    return (direction, dot_new)


def solution(mesh):
    placed = (
        P(None, None, "ga"),
        P("groups", None, None, "ga"),
        P("groups", None, None, "ga"),
        P("ga"),
        P("groups", None),
    )
    return jax.shard_map(
        on_device,
        mesh=mesh,
        in_specs=placed,
        out_specs=(P("groups", None, None, "ga"), P("groups", None)),
        check_vma=False,
    )
```

profile of v0, /device:TPU:0, one launch (start us, length us, event | category | flops | bytes accessed | tf_op | source)
XLA Modules:
  0.0 279.0 jit_solution(1500607859630223277)
XLA Ops:
  7.2 0.0 all-reduce.3.cloned.1.call-start
  7.2 13.1 %fusion.10 = f32[2,2,2,1024,128]{3,4,1,2,0:T(8,128)S(1)} fusion(f32[2,1024,768]{2,1,0:T(8,128)} %param.5, f32[2,2,128,768]{3,2,1,0:T(8,128)} %param.6), kind=kOutput, calls=%fused_computation.12 | convolution fusion | flops 9663676416 | bytes 12058624 | tf_op jit(solution)/shard_map/hng,pcbg->phcnb/dot_general | solution.py:15
  20.4 0.2 fusion.31
  20.5 0.2 fusion.33
  20.7 1.4 pad_maximum_fusion.2
  22.2 0.2 all-reduce.5.cloned.1.call-start
  22.4 0.4 copy-done.3
  22.8 100.4 %all-reduce.3.cloned.1.call-done = f32[2,2,1024,128]{2,3,0,1:T(8,128)} async-done(((f32[2,2,1024,128]{2,3,0,1:T(8,128)}), f32[2,2,1024,128]{2,3,0,1:T(8,128)}) %all-reduce.3.cloned.1.call-update) | async-done | bytes 2097168 | tf_op jit(solution)/shard_map/psum | solution.py:34
  123.2 1.9 slice_negate_fusion.1
  125.2 0.5 maximum_bitcast_fusion
  125.7 0.9 copy-done
  126.6 16.2 %bitcast_subtract_fusion.1 = f32[2,2,128,768]{3,2,1,0:T(8,128)S(1)} fusion(f32[2,2,128,768]{3,2,1,0:T(8,128)S(1)} %copy-done, f32[2,1024,768]{2,1,0:T(8,128)} %param.5, f32[2,1,2,1024,128]{3,4,0,2,1:T(8,128)S(1)} %get-tuple-element.11, f32[2,1,2,1024,128]{3,4,0,2,1:T(8,128)S(1)} %get-tuple-element.10), kind=kOutput, calls=%fused_computation.24 | convolution fusion | flops 9665118208 | bytes 13631488 | tf_op jit(solution)/shard_map/pchnb,hng->pcbg/dot_general | solution.py:28
  142.8 10.2 %fusion.13 = f32[2,2,2,1024,128]{3,4,1,2,0:T(8,128)S(1)} fusion(f32[2,1024,768]{2,1,0:T(8,128)S(1)} %bitcast.84, f32[2,2,128,768]{3,2,1,0:T(8,128)S(1)} %bitcast_subtract_fusion.1, f32[768]{0:T(1024)S(1)} %add_divide_fusion), kind=kOutput, calls=%fused_computation.13 | convolution fusion | flops 9664069632 | bytes 12061696 | tf_op jit(solution)/shard_map/hng,pcbg->phcnb/dot_general | solution.py:15
  153.0 0.2 fusion.28
  153.1 0.2 fusion.30
  153.3 1.4 pad_maximum_fusion.3
  154.7 0.0 all-reduce.5.cloned.1.call-update
  154.8 0.2 fusion.37
  155.0 31.1 %psum.23 = f32[2,128]{1,0:T(2,128)S(1)} all-reduce(f32[2,128]{1,0:T(2,128)S(1)} %fusion.37), channel_id=1, replica_groups=mesh['groups'=2,'ga'=16] {'ga'}, use_global_device_ids=true, to_apply=%region_3.0 | all-reduce | flops 256 | bytes 2048 | tf_op jit(solution)/shard_map/psum | solution.py:39
  186.1 66.3 %all-reduce.5.cloned.1.call-done = f32[2,2,1024,128]{2,3,0,1:T(8,128)} async-done(((f32[2,2,1024,128]{2,3,0,1:T(8,128)}), f32[2,2,1024,128]{2,3,0,1:T(8,128)}) %all-reduce.5.cloned.1.call-update) | async-done | bytes 2097168 | tf_op jit(solution)/shard_map/psum | solution.py:39
  252.5 1.9 slice_negate_fusion
  254.4 0.5 maximum_bitcast_fusion.2
  254.9 0.9 copy-done.1
  255.8 16.4 %fusion.18 = f32[2,2,128,768]{3,2,1,0:T(8,128)} fusion(f32[2,2,128,768]{3,2,1,0:T(8,128)S(1)} %copy-done.1, f32[2,1024,768]{2,1,0:T(8,128)} %param.5, f32[2,2,128,768]{3,2,1,0:T(8,128)S(1)} %bitcast_subtract_fusion.1, f32[2,128]{1,0:T(2,128)S(1)} %div.7, f32[768]{0:T(1024)S(1)} %add_divide_fusion, f32[2,1,2,1024,128]{3,4,0,2,1:T(8,128)S(1)} %get-tuple-element.9, ...), kind=kOutput, calls=%fused_computation.23 | convolution fusion | flops 9666297856 | bytes 15208448 | tf_op jit(solution)/shard_map/pchnb,hng->pcbg/dot_general | solution.py:28
  (15 shorter events, 0.1 us)
Async XLA Ops:
  7.2 116.1 %all-reduce.3.cloned.1.call-start = ((), (), s32[]{:S(2)}) async-start(), calls=%async_computation | async-start | bytes 4194304 | tf_op jit(solution)/shard_map/psum | solution.py:34
  22.1 0.7 copy-start.3
  22.2 230.3 %all-reduce.5.cloned.1.call-start = ((), (), s32[]{:S(2)}) async-start(), calls=%async_computation.1 | async-start | bytes 4194304 | tf_op jit(solution)/shard_map/psum | solution.py:39
  125.1 1.4 copy-start
  125.1 17.6 %slice-start = ((s8[6291456]{0:T(1024)(128)(4,1)}), s8[4194304]{0:T(1024)(128)(4,1)S(1)}, s32[]{:S(2)}) async-start(s8[6291456]{0:T(1024)(128)(4,1)} %bitcast.83), calls=%async_computation.2 | async-start | bytes 8388608
  126.5 16.2 %slice-start.1 = ((s8[6291456]{0:T(1024)(128)(4,1)}), s8[2097152]{0:T(1024)(128)(4,1)S(1)}, s32[]{:S(2)}) async-start(s8[6291456]{0:T(1024)(128)(4,1)} %bitcast.83), calls=%async_computation.3 | async-start | bytes 4194304
  154.7 31.4 %copy-start.4 = (f32[2,128]{1,0:T(2,128)S(1)}, f32[2,128]{1,0:T(2,128)}, u32[]{:S(2)}) copy-start(f32[2,128]{1,0:T(2,128)} %param.9) | copy-start | bytes 3076
  186.1 68.3 %copy-start.2 = (f32[2,128]{1,0:T(2,128)}, f32[2,128]{1,0:T(2,128)S(1)}, u32[]{:S(2)}) copy-start(f32[2,128]{1,0:T(2,128)S(1)} %psum.23) | copy-start | bytes 3076
  254.4 1.4 copy-start.1
Sparse Core Ops, SparseCore 0:
  22.3 100.8 all-reduce.2
  154.9 97.5 all-reduce.4
where the time goes:
time: 279 us
  waiting for transfers between devices  167 us (60%)
  matrix products  55.9 us (20%)
  blocking collectives  31.1 us (11%)
  between operations  14.2 us (5%)
  other arithmetic  8.56 us (3%)
    psum x1, waiting for transfers between devices, on_device(): first_total = lax.psum(first, 'ga')  100 us
    psum x1, waiting for transfers between devices, on_device(): second_total, dot_new = lax.psum((second, local_dot), 'ga')  66.3 us
    dot_general x2, matrix products, correction(): jnp.einsum('pchnb,hng->pcbg', coefficient, occ_rows, precision=highest)  32.6 us
    psum x1, blocking collectives, on_device(): second_total, dot_new = lax.psum((second, local_dot), 'ga')  31.1 us
    dot_general x2, matrix products, margins(): jnp.einsum('hng,pcbg->phcnb', occupied, vectors, precision=highest)  23.3 us
  transfers between devices with their start and end apart: 2, of which 2 were waited for; matrix products, arithmetic and copies ran while one was open for 0% of the time, Pallas kernels for 0%

commit v1 on v0

--- a/solution.py
+++ b/solution.py
@@ -4,6 +4,19 @@
 from jax.sharding import PartitionSpec as P
 
 highest = lax.Precision.HIGHEST
+
+
+def values_register(inner_x):
+    how_many = lax.axis_size("ga")
+    value_now, mixed_arr = (inner_x, 0)
+    while 1 << mixed_arr < how_many:
+        piece_now = range(how_many)
+        front = map(lambda hop_no: (hop_no, hop_no ^ 1 << mixed_arr), piece_now)
+        finding = list(front)
+        top = lax.ppermute(value_now, axis_name="ga", perm=finding)
+        value_now = value_now + top
+        mixed_arr = mixed_arr + 1
+    return value_now
 
 
 def teter_factor(ratio):
@@ -31,7 +44,7 @@
 def on_device(occupied, residual, old_direction, kin_ratio, old_dot):
     factor = teter_factor(kin_ratio)
     first = margins(occupied, residual)
-    first_total = lax.psum(first, "ga")
+    first_total = values_register(first)
     gradient = residual - correction(first_total, occupied)
     precond = factor * gradient
     local_dot = jnp.sum(factor * (gradient[:, 0] ** 2 + gradient[:, 1] ** 2), axis=-1)

time: 279 us -> 368 us (1.32)
  waiting for transfers between devices: 167 us -> 250 us
  starting transfers between devices: 0.26 us -> 8.02 us
  matrix products: 55.9 us -> 50.6 us
    ppermute x0 -> x4, waiting for transfers between devices: none -> 184 us  [values_register(): top = lax.ppermute(value_now, axis_name='ga', perm=finding)]
    psum x1 -> x0, waiting for transfers between devices: 100 us -> none  [on_device(): first_total = lax.psum(first, 'ga')]
    ppermute x0 -> x4, starting transfers between devices: none -> 7.99 us  [values_register(): top = lax.ppermute(value_now, axis_name='ga', perm=finding)]
    dot_general x2, matrix products: 32.6 us -> 27.1 us  [correction(): jnp.einsum('pchnb,hng->pcbg', coefficient, occ_rows, precision=highest)]
  transfers between devices with their start and end apart: 2 -> 5, of which waited for: 2 -> 5; matrix products, arithmetic and copies ran while one was open for 0% -> 0% of each run, Pallas kernels for 0% -> 0%
where the time goes in v1:
time: 368 us; the launch traced here: 367 us
  waiting for transfers between devices  250 us (68%)
  matrix products  50.6 us (14%)
  blocking collectives  33.6 us (9%)
  between operations  14.2 us (4%)
  starting transfers between devices  8.02 us (2%)
  other arithmetic  7.91 us (2%)
    ppermute x4, waiting for transfers between devices, values_register(): top = lax.ppermute(value_now, axis_name='ga', perm=finding)  184 us
    psum x1, waiting for transfers between devices, on_device(): second_total, dot_new = lax.psum((second, local_dot), 'ga')  65.5 us
    psum x1, blocking collectives, on_device(): second_total, dot_new = lax.psum((second, local_dot), 'ga')  33.6 us
    dot_general x2, matrix products, correction(): jnp.einsum('pchnb,hng->pcbg', coefficient, occ_rows, precision=highest)  27.1 us
    dot_general x2, matrix products, margins(): jnp.einsum('hng,pcbg->phcnb', occupied, vectors, precision=highest)  23.5 us
    ppermute x4, starting transfers between devices, values_register(): top = lax.ppermute(value_now, axis_name='ga', perm=finding)  7.99 us
  transfers between devices with their start and end apart: 5, of which 5 were waited for; matrix products, arithmetic and copies ran while one was open for 0% of the time, Pallas kernels for 0%

profile of v1, /device:TPU:0, one launch (start us, length us, event | category | flops | bytes accessed | tf_op | source)
XLA Modules:
  0.0 367.4 jit_solution(79875686517020440)
XLA Ops:
  7.2 13.3 %fusion.10 = f32[2,2,2,1024,128]{3,4,1,2,0:T(8,128)S(1)} fusion(f32[2,1024,768]{2,1,0:T(8,128)} %param.5, f32[2,2,128,768]{3,2,1,0:T(8,128)} %param.6), kind=kOutput, calls=%fused_computation.12 | convolution fusion | flops 9663676416 | bytes 12058624 | tf_op jit(solution)/shard_map/hng,pcbg->phcnb/dot_general | solution.py:28
  21.2 0.6 collective-permute-start
  21.7 3.8 %collective-permute-done = f32[2,2,1024,128]{2,3,0,1:T(8,128)S(1)} collective-permute-done((f32[2,2,1024,128]{2,3,0,1:T(8,128)S(1)}, f32[2,2,1024,128]{2,3,0,1:T(8,128)S(1)}, u32[]{:S(2)}, u32[]{:S(2)}) %collective-permute-start) | collective-permute-done | bytes 2097184 | tf_op jit(solution)/shard_map/ppermute | solution.py:16
  25.5 0.4 fusion.43
  25.9 2.9 collective-permute-start.1
  28.8 45.9 %collective-permute-done.1 = f32[2,2,1024,128]{2,3,0,1:T(8,128)S(1)} collective-permute-done((f32[2,2,1024,128]{2,3,0,1:T(8,128)S(1)}, f32[2,2,1024,128]{2,3,0,1:T(8,128)S(1)}, u32[]{:S(2)}, u32[]{:S(2)}) %collective-permute-start.1) | collective-permute-done | bytes 2097184 | tf_op jit(solution)/shard_map/ppermute | solution.py:16
  74.7 0.9 fusion.44
  75.6 1.9 collective-permute-start.2
  77.5 45.3 %collective-permute-done.2 = f32[2,2,1024,128]{2,3,0,1:T(8,128)S(1)} collective-permute-done((f32[2,2,1024,128]{2,3,0,1:T(8,128)S(1)}, f32[2,2,1024,128]{2,3,0,1:T(8,128)S(1)}, u32[]{:S(2)}, u32[]{:S(2)}) %collective-permute-start.2) | collective-permute-done | bytes 2097184 | tf_op jit(solution)/shard_map/ppermute | solution.py:16
  123.2 2.6 collective-permute-start.3
  125.8 89.5 %collective-permute-done.3 = f32[2,2,1024,128]{2,3,0,1:T(8,128)S(1)} collective-permute-done((f32[2,2,1024,128]{2,3,0,1:T(8,128)S(1)}, f32[2,2,1024,128]{2,3,0,1:T(8,128)S(1)}, u32[]{:S(2)}, u32[]{:S(2)}) %collective-permute-start.3) | collective-permute-done | bytes 2097184 | tf_op jit(solution)/shard_map/ppermute | solution.py:16
  216.1 0.5 maximum_bitcast_fusion
  216.6 0.9 slice-done
  217.5 0.8 slice-done.1
  218.3 0.5 copy-done
  218.8 10.7 %bitcast_subtract_fusion.1 = f32[2,2,128,768]{3,2,1,0:T(8,128)S(1)} fusion(f32[2,2,128,768]{3,2,1,0:T(8,128)S(1)} %copy-done, f32[2,1024,768]{2,1,0:T(8,128)S(1)} %bitcast.84, f32[2,1,2,1024,128]{3,4,0,2,1:T(8,128)S(1)} %get-tuple-element.11, f32[2,1,2,1024,128]{3,4,0,2,1:T(8,128)S(1)} %get-tuple-element.10), kind=kOutput, calls=%fused_computation.24 | convolution fusion | flops 9665118208 | bytes 13631488 | tf_op jit(solution)/shard_map/pchnb,hng->pcbg/dot_general | solution.py:41
  229.5 10.2 %fusion.13 = f32[2,2,2,1024,128]{3,4,1,2,0:T(8,128)S(1)} fusion(f32[2,1024,768]{2,1,0:T(8,128)S(1)} %bitcast.84, f32[2,2,128,768]{3,2,1,0:T(8,128)S(1)} %bitcast_subtract_fusion.1, f32[768]{0:T(1024)S(1)} %add_divide_fusion), kind=kOutput, calls=%fused_computation.13 | convolution fusion | flops 9664069632 | bytes 12061696 | tf_op jit(solution)/shard_map/hng,pcbg->phcnb/dot_general | solution.py:28
  240.0 1.5 pad_maximum_fusion.3
  241.7 33.6 %psum.15 = f32[2,128]{1,0:T(2,128)S(1)} all-reduce(f32[2,128]{1,0:T(2,128)S(1)} %fusion.37), channel_id=1, replica_groups=mesh['groups'=2,'ga'=16] {'ga'}, use_global_device_ids=true, to_apply=%region_2.0 | all-reduce | flops 256 | bytes 2048 | tf_op jit(solution)/shard_map/psum | solution.py:52
  275.3 65.5 %all-reduce.2.cloned.1.call-done = f32[2,2,1024,128]{2,3,0,1:T(8,128)} async-done(((f32[2,2,1024,128]{2,3,0,1:T(8,128)}), f32[2,2,1024,128]{2,3,0,1:T(8,128)}) %all-reduce.2.cloned.1.call-update) | async-done | bytes 2097168 | tf_op jit(solution)/shard_map/psum | solution.py:52
  340.8 1.9 slice_negate_fusion
  342.8 0.5 maximum_bitcast_fusion.2
  343.3 0.9 copy-done.1
  344.2 16.4 %fusion.18 = f32[2,2,128,768]{3,2,1,0:T(8,128)} fusion(f32[2,2,128,768]{3,2,1,0:T(8,128)S(1)} %copy-done.1, f32[2,1024,768]{2,1,0:T(8,128)} %param.5, f32[2,2,128,768]{3,2,1,0:T(8,128)S(1)} %bitcast_subtract_fusion.1, f32[2,128]{1,0:T(2,128)S(1)} %div.7, f32[768]{0:T(1024)S(1)} %add_divide_fusion, f32[2,1,2,1024,128]{3,4,0,2,1:T(8,128)S(1)} %get-tuple-element.9, ...), kind=kOutput, calls=%fused_computation.23 | convolution fusion | flops 9666297856 | bytes 15208448 | tf_op jit(solution)/shard_map/pchnb,hng->pcbg/dot_general | solution.py:41
  (24 shorter events, 2.4 us)
Async XLA Ops:
  7.2 333.7 %all-reduce.2.cloned.1.call-start = ((), (), s32[]{:S(2)}) async-start(), calls=%async_computation | async-start | bytes 4194304 | tf_op jit(solution)/shard_map/psum | solution.py:52
  21.2 4.3 %collective-permute-start = (f32[2,2,1024,128]{2,3,0,1:T(8,128)S(1)}, f32[2,2,1024,128]{2,3,0,1:T(8,128)S(1)}, u32[]{:S(2)}, u32[]{:S(2)}) collective-permute-start(f32[2,2,1024,128]{2,3,0,1:T(8,128)S(1)} %pad_maximum_fusion.2), channel_id=1, source_target_pairs={{0,1},{1,0},{2,3},{3,2},{4,5},{5,4},{6,7},{7,6},{8,9},{9,8},{10,11... | collective-permute-start | bytes 6291464 | tf_op jit(solution)/shard_map/ppermute | solution.py:16
  25.9 48.8 %collective-permute-start.1 = (f32[2,2,1024,128]{2,3,0,1:T(8,128)S(1)}, f32[2,2,1024,128]{2,3,0,1:T(8,128)S(1)}, u32[]{:S(2)}, u32[]{:S(2)}) collective-permute-start(f32[2,2,1024,128]{2,3,0,1:T(8,128)S(1)} %fusion.43), channel_id=1, source_target_pairs={{0,2},{1,3},{2,0},{3,1},{4,6},{5,7},{6,4},{7,5},{8,10},{9,11},{10,... | collective-permute-start | bytes 6291464 | tf_op jit(solution)/shard_map/ppermute | solution.py:16
  75.6 50.2 %copy-start.3 = (f32[768]{0:T(1024)S(1)}, f32[768]{0:T(1024)}, u32[]{:S(2)}) copy-start(f32[768]{0:T(1024)} %param.8) | copy-start | bytes 9220
  75.6 47.2 %collective-permute-start.2 = (f32[2,2,1024,128]{2,3,0,1:T(8,128)S(1)}, f32[2,2,1024,128]{2,3,0,1:T(8,128)S(1)}, u32[]{:S(2)}, u32[]{:S(2)}) collective-permute-start(f32[2,2,1024,128]{2,3,0,1:T(8,128)S(1)} %fusion.44), channel_id=1, source_target_pairs={{0,4},{1,5},{2,6},{3,7},{4,0},{5,1},{6,2},{7,3},{8,12},{9,13},{10,... | collective-permute-start | bytes 6291464 | tf_op jit(solution)/shard_map/ppermute | solution.py:16
  123.2 92.1 %collective-permute-start.3 = (f32[2,2,1024,128]{2,3,0,1:T(8,128)S(1)}, f32[2,2,1024,128]{2,3,0,1:T(8,128)S(1)}, u32[]{:S(2)}, u32[]{:S(2)}) collective-permute-start(f32[2,2,1024,128]{2,3,0,1:T(8,128)S(1)} %add.75), channel_id=1, source_target_pairs={{0,8},{1,9},{2,10},{3,11},{4,12},{5,13},{6,14},{7,15},{8,0},{9,1},... | collective-permute-start | bytes 6291464 | tf_op jit(solution)/shard_map/ppermute | solution.py:16
  215.3 2.2 slice-start
  215.7 2.6 slice-start.1
  216.1 2.7 copy-start
  241.5 33.8 %copy-start.4 = (f32[2,128]{1,0:T(2,128)S(1)}, f32[2,128]{1,0:T(2,128)}, u32[]{:S(2)}) copy-start(f32[2,128]{1,0:T(2,128)} %param.9) | copy-start | bytes 3076
  275.3 67.4 %copy-start.2 = (f32[2,128]{1,0:T(2,128)}, f32[2,128]{1,0:T(2,128)S(1)}, u32[]{:S(2)}) copy-start(f32[2,128]{1,0:T(2,128)S(1)} %psum.15) | copy-start | bytes 3076
  342.8 1.4 copy-start.1
Sparse Core Ops, SparseCore 0:
  241.7 99.1 all-reduce.1
